TPU v7x, 32 devices: a whole 2x2x4 slice. The times are simulated.
32 devices in a mesh: wide: 16 (over z, x, core), narrow: 2 (over y).
Axes of the slice: x: 2, y: 2, z: 4, core: 2. Of those that a mesh axis runs over, the one named last changes fastest.
Arguments:
- layer_in: bfloat16 [16384, 768], P(('wide', 'narrow')), may hold values from -6 to 6
- doc_ids: int32 [32, 512], P('wide'), may hold values from 0 to 3, never falling along the last dimension, each value on 1 to 256 neighbouring positions
- query_weight: bfloat16 [768, 768], P(('wide', 'narrow')), may hold values from -0.21875 to 0.21875
- query_bias: bfloat16 [768], P(('wide', 'narrow')), may hold values from -2 to 2
- key_weight: bfloat16 [768, 768], P(('wide', 'narrow')), may hold values from -0.21875 to 0.21875
- key_bias: bfloat16 [768], P(('wide', 'narrow')), may hold values from -2 to 2
- value_weight: bfloat16 [768, 768], P(('wide', 'narrow')), may hold values from -0.21875 to 0.21875
- value_bias: bfloat16 [768], P(('wide', 'narrow')), may hold values from -2 to 2
- output_weight: bfloat16 [768, 768], P(('wide', 'narrow')), may hold values from -0.875 to 0.875
- output_bias: bfloat16 [768], P(('wide', 'narrow')), may hold values from -2 to 2
- attn_gain: bfloat16 [768], P(('wide', 'narrow')), may hold values from 0.25 to 1.75
- attn_shift: bfloat16 [768], P(('wide', 'narrow')), may hold values from -2 to 2
- inner_weight: bfloat16 [768, 3072], P('wide', 'narrow'), may hold values from -0.21875 to 0.21875
- inner_bias: bfloat16 [3072], P(('narrow', 'wide')), may hold values from -2 to 2
- outer_weight: bfloat16 [3072, 768], P('narrow', 'wide'), may hold values from -0.109375 to 0.109375
- outer_bias: bfloat16 [768], P(('wide', 'narrow')), may hold values from -2 to 2
- ffn_gain: bfloat16 [768], P(('wide', 'narrow')), may hold values from 0.25 to 1.75
- ffn_shift: bfloat16 [768], P(('wide', 'narrow')), may hold values from -2 to 2
- cotangent: bfloat16 [16384, 768], P(('wide', 'narrow')), may hold values from -6 to 6
Outputs:
- layer_out: float32 [16384, 768], P(('wide', 'narrow'))
- input_grad: float32 [16384, 768], P(('wide', 'narrow'))
- query_wgrad: float32 [768, 768], P(('wide', 'narrow'))
- query_bgrad: float32 [768], P(('wide', 'narrow'))
- key_wgrad: float32 [768, 768], P(('wide', 'narrow'))
- key_bgrad: float32 [768], P(('wide', 'narrow'))
- value_wgrad: float32 [768, 768], P(('wide', 'narrow'))
- value_bgrad: float32 [768], P(('wide', 'narrow'))
- output_wgrad: float32 [768, 768], P(('wide', 'narrow'))
- output_bgrad: float32 [768], P(('wide', 'narrow'))
- attn_ggrad: float32 [768], P(('wide', 'narrow'))
- attn_sgrad: float32 [768], P(('wide', 'narrow'))
- inner_wgrad: float32 [768, 3072], P('wide', 'narrow')
- inner_bgrad: float32 [3072], P(('narrow', 'wide'))
- outer_wgrad: float32 [3072, 768], P('narrow', 'wide')
- outer_bgrad: float32 [768], P(('wide', 'narrow'))
- ffn_ggrad: float32 [768], P(('wide', 'narrow'))
- ffn_sgrad: float32 [768], P(('wide', 'narrow'))
Inputs may be any that keep to these rules, and one draw needn't show every extreme that they name: `doc_ids`: within each pack the ids never fall, so each document is one run of 1 to 256 tokens.
All inputs are finite; a program needn't handle non-finite values.
Results may differ from a plain program's by a relative error of at most 0.018.
Values may be sent and summed in bfloat16 or wider, within the bound.
A program may use at most 192 MiB of HBM per device.

v0:
```python
import jax
import jax.numpy as jnp
from jax import lax
from jax.sharding import PartitionSpec as P

D = 768
HEADS = 12
HEAD_DIM = 64


layer_eps = 1e-12
masked_score = -1e30


def swapped(shard, axis, bit):
    return lax.ppermute(shard, axis, [(i, i ^ 1 << bit) for i in range(lax.axis_size(axis))])


def layer_norm(values, gain_vec, shift_vec):
    center = values - jnp.mean(values, axis=-1, keepdims=True)
    spread = jnp.mean(center * center, axis=-1, keepdims=True)
    return center * lax.rsqrt(spread + layer_eps) * gain_vec + shift_vec


def gelu_exact(values):
    return jax.nn.gelu(values, approximate=False)


def rotary_tables(doc_row):
    places = jnp.arange(doc_row.shape[0], dtype=jnp.int32)
    before = jnp.sum((doc_row[None, :] < doc_row[:, None]).astype(jnp.int32), axis=1)
    position = (places - before).astype(jnp.float32)
    frequency = 10000.0 ** (-2.0 * jnp.arange(HEAD_DIM // 2, dtype=jnp.float32) / HEAD_DIM)
    angles = position[:, None] * frequency[None, :]
    return (jnp.cos(angles), jnp.sin(angles))


def rotate(values, cosine, sine_tab):
    half_dim = values.shape[-1] // 2
    first_half = values[..., :half_dim]
    second = values[..., half_dim:]
    return jnp.concatenate(
        [first_half * cosine - second * sine_tab, second * cosine + first_half * sine_tab], axis=-1
    )


def unrotate(values, cosine, sine_tab):
    half_dim = values.shape[-1] // 2
    first_half = values[..., :half_dim]
    second = values[..., half_dim:]
    return jnp.concatenate(
        [first_half * cosine + second * sine_tab, second * cosine - first_half * sine_tab], axis=-1
    )


def contract_rows(left_op, right_op):
    return lax.dot_general(
        left_op, right_op, (((0,), (0,)), ((), ())), preferred_element_type=jnp.float32
    )


def contract_cols(left_op, right_op):
    return lax.dot_general(
        left_op, right_op, (((1,), (1,)), ((), ())), preferred_element_type=jnp.float32
    )


def score_block(query_rot, key_rot, query_docs, key_docs):
    scores = jnp.einsum(
        "qhd,khd->hqk", query_rot, key_rot, preferred_element_type=jnp.float32
    ) * HEAD_DIM ** (-0.5)
    same_doc = query_docs[:, None] == key_docs[None, :]
    return jnp.where(same_doc[None], scores, masked_score)


def attend_pack(packed):
    query_rot, key_rot, value_low, query_docs, key_docs = packed
    scores = score_block(query_rot, key_rot, query_docs, key_docs)
    row_peak = jnp.max(scores, axis=-1, keepdims=True)
    exponent = jnp.exp(scores - row_peak)
    totals = jnp.sum(exponent, axis=-1, keepdims=True)
    probability = (exponent / totals).astype(jnp.bfloat16)
    mixed_out = jnp.einsum(
        "hqk,khd->qhd", probability, value_low, preferred_element_type=jnp.float32
    )
    return (mixed_out, row_peak + jnp.log(totals))


def attend_back(packed):
    query_rot, key_rot, value_low, query_docs, key_docs, logsum, grad_mixed = packed
    probability = jnp.exp(score_block(query_rot, key_rot, query_docs, key_docs) - logsum)
    grad_values = jnp.einsum(
        "hqk,qhd->khd",
        probability.astype(jnp.bfloat16),
        grad_mixed,
        preferred_element_type=jnp.float32,
    )
    grad_probs = jnp.einsum(
        "qhd,khd->hqk", grad_mixed, value_low, preferred_element_type=jnp.float32
    )
    inner_sum = jnp.sum(probability * grad_probs, axis=-1, keepdims=True)
    grad_scores = (probability * (grad_probs - inner_sum)).astype(jnp.bfloat16)
    grad_query = jnp.einsum(
        "hqk,khd->qhd", grad_scores, key_rot, preferred_element_type=jnp.float32
    ) * HEAD_DIM ** (-0.5)
    grad_keys = jnp.einsum(
        "hqk,qhd->khd", grad_scores, query_rot, preferred_element_type=jnp.float32
    ) * HEAD_DIM ** (-0.5)
    return (grad_query, grad_keys, grad_values)


def local(
    layer_in,
    doc_ids,
    query_weight,
    query_bias,
    key_weight,
    key_bias,
    value_weight,
    value_bias,
    output_weight,
    output_bias,
    attn_gain,
    attn_shift,
    inner_weight,
    inner_bias,
    outer_weight,
    outer_bias,
    ffn_gain,
    ffn_shift,
    cotangent,
):
    shared = (
        lax.all_gather(query_weight, ("wide", "narrow"), axis=0, tiled=True),
        lax.all_gather(key_weight, ("wide", "narrow"), axis=0, tiled=True),
        lax.all_gather(value_weight, ("wide", "narrow"), axis=0, tiled=True),
        lax.all_gather(output_weight, ("wide", "narrow"), axis=0, tiled=True),
        lax.all_gather(query_bias, ("wide", "narrow"), axis=0, tiled=True),
        lax.all_gather(key_bias, ("wide", "narrow"), axis=0, tiled=True),
        lax.all_gather(value_bias, ("wide", "narrow"), axis=0, tiled=True),
        lax.all_gather(output_bias, ("wide", "narrow"), axis=0, tiled=True),
        lax.all_gather(attn_gain, ("wide", "narrow"), axis=0, tiled=True),
        lax.all_gather(attn_shift, ("wide", "narrow"), axis=0, tiled=True),
        lax.all_gather(outer_bias, ("wide", "narrow"), axis=0, tiled=True),
        lax.all_gather(ffn_gain, ("wide", "narrow"), axis=0, tiled=True),
        lax.all_gather(ffn_shift, ("wide", "narrow"), axis=0, tiled=True),
    )
    query_full, key_full, value_full, output_full = (shared[0], shared[1], shared[2], shared[3])
    (
        query_offset,
        key_offset,
        value_offset,
        output_offset,
        attn_scale,
        attn_offset,
        outer_offset,
        ffn_scale,
        ffn_offset,
    ) = [piece.astype(jnp.float32) for piece in shared[4:]]
    inner_cols, outer_rows, inner_offset = (
        lax.all_gather(inner_weight, "wide", axis=0, tiled=True),
        lax.all_gather(outer_weight, "wide", axis=1, tiled=True),
        lax.all_gather(inner_bias, "wide", axis=0, tiled=True),
    )
    rows_dev = layer_in.shape[0]
    half_len = doc_ids.shape[1] // 2
    pack_count = rows_dev // half_len
    narrow_place = lax.axis_index("narrow")
    half_bit = narrow_place % 2
    pair_slot = narrow_place // 2
    pack_docs = lax.dynamic_slice_in_dim(doc_ids, pair_slot * pack_count, pack_count, 0)
    cosine, sine_tab = jax.vmap(rotary_tables)(pack_docs)
    cosine = cosine[:, :, None, :]
    sine_tab = sine_tab[:, :, None, :]
    own_start = half_bit * half_len
    far_start = (1 - half_bit) * half_len
    own_cos = lax.dynamic_slice_in_dim(cosine, own_start, half_len, 1)
    own_sin = lax.dynamic_slice_in_dim(sine_tab, own_start, half_len, 1)
    own_docs = lax.dynamic_slice_in_dim(pack_docs, own_start, half_len, 1)
    far_docs = lax.dynamic_slice_in_dim(pack_docs, far_start, half_len, 1)
    key_docs = jnp.concatenate([own_docs, far_docs], axis=1)

    def heads_of(values):
        return values.reshape(pack_count, half_len, HEADS, HEAD_DIM)

    def project(rows, weight, offset_vec):
        return jnp.dot(rows, weight, preferred_element_type=jnp.float32) + offset_vec

    query_rot = rotate(
        heads_of(project(layer_in, query_full, query_offset)), own_cos, own_sin
    ).astype(jnp.bfloat16)
    key_rot = rotate(heads_of(project(layer_in, key_full, key_offset)), own_cos, own_sin).astype(
        jnp.bfloat16
    )
    value_low = heads_of(project(layer_in, value_full, value_offset)).astype(jnp.bfloat16)
    far_keys, far_values = swapped((key_rot, value_low), "narrow", 0)
    all_keys = jnp.concatenate([key_rot, far_keys], axis=1)
    all_values = jnp.concatenate([value_low, far_values], axis=1)
    mixed_out, logsum = lax.map(attend_pack, (query_rot, all_keys, all_values, own_docs, key_docs))
    mixed_low = mixed_out.reshape(rows_dev, D).astype(jnp.bfloat16)
    attn_out = jnp.dot(mixed_low, output_full, preferred_element_type=jnp.float32) + output_offset
    res_one = layer_in.astype(jnp.float32) + attn_out
    norm_one, norm_pull = jax.vjp(layer_norm, res_one, attn_scale, attn_offset)
    norm_low = norm_one.astype(jnp.bfloat16)
    group_rows = lax.all_gather(norm_low, "narrow", axis=0, tiled=True)
    inner_pre = jnp.dot(
        group_rows, inner_cols, preferred_element_type=jnp.float32
    ) + inner_offset.astype(jnp.float32)
    act_value, gelu_pull = jax.vjp(gelu_exact, inner_pre)
    act_low = act_value.astype(jnp.bfloat16)
    block_rows = act_low
    outer_out = (
        lax.psum_scatter(
            jnp.dot(block_rows, outer_rows, preferred_element_type=jnp.float32),
            "narrow",
            scatter_dimension=0,
            tiled=True,
        )
        + outer_offset
    )
    res_two = norm_one + outer_out
    layer_out, ffn_pull = jax.vjp(layer_norm, res_two, ffn_scale, ffn_offset)
    grad_two, ffn_gsum, ffn_ssum = ffn_pull(cotangent.astype(jnp.float32))
    grad_outer = grad_two.astype(jnp.bfloat16)
    outer_bsum = jnp.sum(grad_outer.astype(jnp.float32), axis=0)
    group_grads = lax.all_gather(grad_outer, "narrow", axis=0, tiled=True)
    grad_act = contract_cols(group_grads, outer_rows)
    grad_inner = gelu_pull(grad_act)[0].astype(jnp.bfloat16)
    outer_wsum = contract_rows(act_low, group_grads)
    inner_wsum = contract_rows(group_rows, grad_inner)
    inner_bsum = jnp.sum(grad_inner.astype(jnp.float32), axis=0)
    block_rows = grad_inner
    grad_part = lax.psum_scatter(
        contract_cols(block_rows, inner_cols), "narrow", scatter_dimension=0, tiled=True
    )
    inner_wgrad, outer_wgrad, inner_bgrad = (
        lax.psum_scatter(
            inner_wsum.astype(jnp.bfloat16), "wide", scatter_dimension=0, tiled=True
        ).astype(jnp.float32),
        lax.psum_scatter(
            outer_wsum.astype(jnp.bfloat16), "wide", scatter_dimension=1, tiled=True
        ).astype(jnp.float32),
        lax.psum_scatter(
            inner_bsum.astype(jnp.bfloat16), "wide", scatter_dimension=0, tiled=True
        ).astype(jnp.float32),
    )
    grad_norm = grad_two + grad_part
    grad_one, attn_gsum, attn_ssum = norm_pull(grad_norm)
    grad_attn = grad_one.astype(jnp.bfloat16)
    output_bsum = jnp.sum(grad_attn.astype(jnp.float32), axis=0)
    output_wsum = contract_rows(mixed_low, grad_attn)
    grad_mixed = heads_of(contract_cols(grad_attn, output_full).astype(jnp.bfloat16))
    grad_qrot, grad_kall, grad_vall = lax.map(
        attend_back, (query_rot, all_keys, all_values, own_docs, key_docs, logsum, grad_mixed)
    )
    back_keys, back_values = (
        swapped(grad_kall[:, half_len:].astype(jnp.bfloat16), "narrow", 0).astype(jnp.float32),
        swapped(grad_vall[:, half_len:].astype(jnp.bfloat16), "narrow", 0).astype(jnp.float32),
    )
    grad_krot = grad_kall[:, :half_len] + back_keys
    grad_values = (grad_vall[:, :half_len] + back_values).astype(jnp.bfloat16).reshape(rows_dev, D)
    grad_query = unrotate(grad_qrot, own_cos, own_sin).reshape(rows_dev, D).astype(jnp.bfloat16)
    grad_keys = unrotate(grad_krot, own_cos, own_sin).reshape(rows_dev, D).astype(jnp.bfloat16)
    query_wsum = contract_rows(layer_in, grad_query)
    key_wsum = contract_rows(layer_in, grad_keys)
    value_wsum = contract_rows(layer_in, grad_values)
    query_bsum = jnp.sum(grad_query.astype(jnp.float32), axis=0)
    key_bsum = jnp.sum(grad_keys.astype(jnp.float32), axis=0)
    value_bsum = jnp.sum(grad_values.astype(jnp.float32), axis=0)
    input_grad = (
        grad_one
        + contract_cols(grad_query, query_full)
        + contract_cols(grad_keys, key_full)
        + contract_cols(grad_values, value_full)
    )
    summed = (
        lax.psum_scatter(query_wsum, ("wide", "narrow"), scatter_dimension=0, tiled=True),
        lax.psum_scatter(key_wsum, ("wide", "narrow"), scatter_dimension=0, tiled=True),
        lax.psum_scatter(value_wsum, ("wide", "narrow"), scatter_dimension=0, tiled=True),
        lax.psum_scatter(output_wsum, ("wide", "narrow"), scatter_dimension=0, tiled=True),
        lax.psum_scatter(query_bsum, ("wide", "narrow"), scatter_dimension=0, tiled=True),
        lax.psum_scatter(key_bsum, ("wide", "narrow"), scatter_dimension=0, tiled=True),
        lax.psum_scatter(value_bsum, ("wide", "narrow"), scatter_dimension=0, tiled=True),
        lax.psum_scatter(output_bsum, ("wide", "narrow"), scatter_dimension=0, tiled=True),
        lax.psum_scatter(attn_gsum, ("wide", "narrow"), scatter_dimension=0, tiled=True),
        lax.psum_scatter(attn_ssum, ("wide", "narrow"), scatter_dimension=0, tiled=True),
        lax.psum_scatter(outer_bsum, ("wide", "narrow"), scatter_dimension=0, tiled=True),
        lax.psum_scatter(ffn_gsum, ("wide", "narrow"), scatter_dimension=0, tiled=True),
        lax.psum_scatter(ffn_ssum, ("wide", "narrow"), scatter_dimension=0, tiled=True),
    )
    return (
        layer_out,
        input_grad,
        summed[0],
        summed[4],
        summed[1],
        summed[5],
        summed[2],
        summed[6],
        summed[3],
        summed[7],
        summed[8],
        summed[9],
        inner_wgrad,
        inner_bgrad,
        outer_wgrad,
        summed[10],
        summed[11],
        summed[12],
    )


def solution(mesh):
    return jax.shard_map(
        local,
        mesh=mesh,
        in_specs=(
            P(("wide", "narrow"), None),
            P("wide", None),
            P(("wide", "narrow"), None),
            P(("wide", "narrow")),
            P(("wide", "narrow"), None),
            P(("wide", "narrow")),
            P(("wide", "narrow"), None),
            P(("wide", "narrow")),
            P(("wide", "narrow"), None),
            P(("wide", "narrow")),
            P(("wide", "narrow")),
            P(("wide", "narrow")),
            P("wide", "narrow"),
            P(("narrow", "wide")),
            P("narrow", "wide"),
            P(("wide", "narrow")),
            P(("wide", "narrow")),
            P(("wide", "narrow")),
            P(("wide", "narrow"), None),
        ),
        out_specs=(
            P(("wide", "narrow"), None),
            P(("wide", "narrow"), None),
            P(("wide", "narrow"), None),
            P(("wide", "narrow")),
            P(("wide", "narrow"), None),
            P(("wide", "narrow")),
            P(("wide", "narrow"), None),
            P(("wide", "narrow")),
            P(("wide", "narrow"), None),
            P(("wide", "narrow")),
            P(("wide", "narrow")),
            P(("wide", "narrow")),
            P("wide", "narrow"),
            P(("narrow", "wide")),
            P("narrow", "wide"),
            P(("wide", "narrow")),
            P(("wide", "narrow")),
            P(("wide", "narrow")),
        ),
        check_vma=False,
    )
```

profile of v0, /device:TPU:0, one launch (start us, length us, event | category | flops | bytes accessed | tf_op | source)
XLA Modules:
  0.0 1057.9 jit_solution(5921576848460198121)
XLA Ops:
  18.8 42.6 %all-reduce.21 = (bf16[768]{0:T(1024)(128)(2,1)S(1)}, bf16[768]{0:T(1024)(128)(2,1)S(1)}, bf16[768]{0:T(1024)(128)(2,1)S(1)}, bf16[768]{0:T(1024)(128)(2,1)S(1)}...) all-reduce(bf16[768]{0:T(1024)(128)(2,1)S(1)} %dynamic-update-slice, ...), channel_id=1, replica_groups=mesh['wide'=16,'narrow'=2] {'wide','narrow'}, use_global_device_ids=true, to_apply=%add | all-reduce | flops 6912 | bytes 27648
  75.5 48.6 %all-gather.13.cloned.1.call-done = bf16[768,768]{1,0:T(8,128)(2,1)} async-done(((bf16[24,768]{1,0:T(8,128)(2,1)}), bf16[768,768]{1,0:T(8,128)(2,1)}) %all-gather.13.cloned.1.call-update) | async-done | bytes 1179664 | tf_op jit(solution)/shard_map/all_gather | solution.py:135
  137.8 42.3 %all-gather.9.cloned.1.call-done = bf16[768,768]{1,0:T(8,128)(2,1)} async-done(((bf16[24,768]{1,0:T(8,128)(2,1)}), bf16[768,768]{1,0:T(8,128)(2,1)}) %all-gather.9.cloned.1.call-update) | async-done | bytes 1179664 | tf_op jit(solution)/shard_map/all_gather | solution.py:136
  191.8 13.9 %collective-permute-done = bf16[2,256,12,64]{1,0,3,2:T(2,128)(2,1)} collective-permute-done((bf16[2,256,12,64]{1,0,3,2:T(2,128)(2,1)}, bf16[2,256,12,64]{1,0,3,2:T(2,128)(2,1)}, u32[]{:S(2)}, u32[]{:S(2)}) %collective-permute-start) | collective-permute-done | bytes 786464 | tf_op jit(solution)/shard_map/ppermute | solution.py:16
  210.3 13.3 %while.26 = (s32[]{:T(128)}, bf16[2,256,12,64]{1,3,2,0:T(8,128)(2,1)}, f32[2,12,256,1]{2,1,3,0:T(8,128)S(1)}, bf16[2,512,12,64]{1,3,2,0:T(8,128)(2,1)}, s32[2,25...) while((s32[]{:T(128)}, ...), condition=%wide.region_4.5_spmd, body=%wide.region_1.4_spmd.sunk | while | flops 421655552 | bytes 28572804 | solution.py:199
  243.1 33.4 %all-reduce.6 = bf16[1536]{0:T(1024)(128)(2,1)S(1)} all-reduce(bf16[1536]{0:T(1024)(128)(2,1)S(1)} %dynamic-update-slice.6), channel_id=1, replica_groups=mesh['wide'=16,'narrow'=2] {'wide'}, use_global_device_ids=true, to_apply=%add.6 | all-reduce | flops 1536 | bytes 6144
  279.4 28.0 %all-gather.17.cloned.1.call-done = bf16[1024,768]{1,0:T(8,128)(2,1)} async-done(((bf16[512,768]{1,0:T(8,128)(2,1)}), bf16[1024,768]{1,0:T(8,128)(2,1)}) %all-gather.17.cloned.1.call-update) | async-done | bytes 1572880 | tf_op jit(solution)/shard_map/all_gather | solution.py:205
  307.4 20.1 %multiply_convert_fusion.1 = (bf16[1024,1536]{1,0:T(8,128)(2,1)}, f32[1024,1536]{1,0:T(8,128)}, f32[1024,1536]{1,0:T(8,128)}) fusion(f32[1536]{0:T(1024)S(1)} %convert_element_type.161, bf16[1024,768]{1,0:T(8,128)(2,1)} %all-gather.17.cloned.1.call-done, bf16[768,1536]{1,0:T(8,128)(2,1)} %all-gather.19.cloned.1.call-done), kind=kOutput, calls=%fused_computation.66 | convolution fusion | flops 2519728128 | bytes 19666944 | tf_op jit(solution)/shard_map/dot_general | solution.py:206
  327.5 24.5 %all-gather.21.cloned.1.call-done = bf16[1536,768]{0,1:T(8,128)(2,1)} async-done(((bf16[1536,48]{0,1:T(8,128)(2,1)}), bf16[1536,768]{0,1:T(8,128)(2,1)}) %all-gather.21.cloned.1.call-update) | async-done | bytes 2359312 | tf_op jit(solution)/shard_map/all_gather | solution.py:162
  359.1 42.2 %reduce-scatter.15.cloned.1.call-done = f32[512,768]{1,0:T(8,128)} async-done(((f32[1024,768]{1,0:T(8,128)}), f32[512,768]{1,0:T(8,128)}) %reduce-scatter.15.cloned.1.call-update) | async-done | bytes 1572880 | tf_op jit(solution)/shard_map/reduce_scatter | solution.py:213
  409.1 27.1 %all-gather.23.cloned.1.call-done = bf16[1024,768]{1,0:T(8,128)(2,1)} async-done(((bf16[512,768]{1,0:T(8,128)(2,1)}), bf16[1024,768]{1,0:T(8,128)(2,1)}) %all-gather.23.cloned.1.call-update) | async-done | bytes 1572880 | tf_op jit(solution)/shard_map/all_gather | solution.py:226
  465.9 30.2 %reduce-scatter.17.cloned.1.call-done = f32[512,768]{1,0:T(8,128)} async-done(((f32[1024,768]{1,0:T(8,128)}), f32[512,768]{1,0:T(8,128)}) %reduce-scatter.17.cloned.1.call-update) | async-done | bytes 1572880 | tf_op jit(solution)/shard_map/reduce_scatter | solution.py:233
  511.7 132.5 %while.27 = (s32[]{:T(128)}, f32[2,256,12,64]{1,0,3,2:T(2,128)}, f32[2,512,12,64]{1,0,3,2:T(2,128)}, f32[2,512,12,64]{1,3,2,0:T(8,128)}, bf16[2,512,12,64]{1,3,2...) while((s32[]{:T(128)}, f32[2,256,12,64]{1,0,3,2:T(2,128)}, ...), condition=%wide.region_17.18_spmd, body=%wide.region_15.17_spmd.sunk | while | flops 1030943744 | bytes 121742712 | solution.py:253
  523.4 28.9 %dynamic_update_slice.30 = f32[2,512,12,64]{1,0,3,2:T(2,128)} dynamic-update-slice(f32[2,512,12,64]{1,0,3,2:T(2,128)} %get-tuple-element.542, f32[1,512,12,64]{1,0,3,2:T(1,128)} %copy.141, s32[]{:T(128)} %get-tuple-element.540, s32[]{:T(128)} %constant.69.clone.1..sunk, s32[]{:T(128)} %constant.69.clone.1..sunk, s32[]{:T(128)} %constant.69.clone.1..sunk) | dynamic-update-slice | bytes 3145732 | tf_op jit(solution)/shard_map/while/body/jit(dynamic_update_index_in_dim)/dynamic_update_slice | solution.py:253
  555.4 16.7 %dynamic_update_slice.29 = f32[2,256,12,64]{1,0,3,2:T(2,128)} dynamic-update-slice(f32[2,256,12,64]{1,0,3,2:T(2,128)} %get-tuple-element.541, f32[1,256,12,64]{1,0,3,2:T(1,128)S(1)} %copy.140, s32[]{:T(128)} %get-tuple-element.540, s32[]{:T(128)} %constant.69.clone.1..sunk, s32[]{:T(128)} %constant.69.clone.1..sunk, s32[]{:T(128)} %constant.69.clone.1..sunk) | dynamic-update-slice | bytes 1572868 | tf_op jit(solution)/shard_map/while/body/jit(dynamic_update_index_in_dim)/dynamic_update_slice | solution.py:199
  589.7 29.0 %dynamic_update_slice.30 = f32[2,512,12,64]{1,0,3,2:T(2,128)} dynamic-update-slice(f32[2,512,12,64]{1,0,3,2:T(2,128)} %get-tuple-element.542, f32[1,512,12,64]{1,0,3,2:T(1,128)} %copy.141, s32[]{:T(128)} %get-tuple-element.540, s32[]{:T(128)} %constant.69.clone.1..sunk, s32[]{:T(128)} %constant.69.clone.1..sunk, s32[]{:T(128)} %constant.69.clone.1..sunk) | dynamic-update-slice | bytes 3145732 | tf_op jit(solution)/shard_map/while/body/jit(dynamic_update_index_in_dim)/dynamic_update_slice | solution.py:253
  621.7 16.7 %dynamic_update_slice.29 = f32[2,256,12,64]{1,0,3,2:T(2,128)} dynamic-update-slice(f32[2,256,12,64]{1,0,3,2:T(2,128)} %get-tuple-element.541, f32[1,256,12,64]{1,0,3,2:T(1,128)S(1)} %copy.140, s32[]{:T(128)} %get-tuple-element.540, s32[]{:T(128)} %constant.69.clone.1..sunk, s32[]{:T(128)} %constant.69.clone.1..sunk, s32[]{:T(128)} %constant.69.clone.1..sunk) | dynamic-update-slice | bytes 1572868 | tf_op jit(solution)/shard_map/while/body/jit(dynamic_update_index_in_dim)/dynamic_update_slice | solution.py:199
  646.2 18.8 %collective-permute-done.3 = bf16[2,256,12,64]{1,3,2,0:T(8,128)(2,1)S(1)} collective-permute-done((bf16[2,256,12,64]{1,3,2,0:T(8,128)(2,1)S(1)}, bf16[2,256,12,64]{1,3,2,0:T(8,128)(2,1)S(1)}, u32[]{:S(2)}, u32[]{:S(2)}) %collective-permute-start.3) | collective-permute-done | bytes 786464 | tf_op jit(solution)/shard_map/ppermute | solution.py:16
  673.6 21.9 %collective-permute-done.2 = bf16[2,256,12,64]{1,0,3,2:T(2,128)(2,1)S(1)} collective-permute-done((bf16[2,256,12,64]{1,0,3,2:T(2,128)(2,1)S(1)}, bf16[2,256,12,64]{1,0,3,2:T(2,128)(2,1)S(1)}, u32[]{:S(2)}, u32[]{:S(2)}) %collective-permute-start.2) | collective-permute-done | bytes 786464 | tf_op jit(solution)/shard_map/ppermute | solution.py:16
  716.8 31.0 %all-reduce.16 = bf16[1536]{0:T(1024)(128)(2,1)S(1)} all-reduce(bf16[1536]{0:T(1024)(128)(2,1)S(1)} %get-tuple-element.327), channel_id=15, replica_groups=mesh['wide'=16,'narrow'=2] {'wide'}, use_global_device_ids=true, to_apply=%region_36.37.clone | all-reduce | flops 1536 | bytes 6144
  752.0 37.7 %all-reduce.20 = (f32[768]{0:T(1024)S(1)}, f32[768]{0:T(1024)S(1)}, f32[768]{0:T(1024)S(1)}, f32[768]{0:T(1024)S(1)}, f32[768]{0:T(1024)S(1)}, /*index=5*/f32[76...) all-reduce(f32[768]{0:T(1024)S(1)} %reduce_sum.240, ...), channel_id=5, replica_groups=mesh['wide'=16,'narrow'=2] {'wide','narrow'}, use_global_device_ids=true, to_apply=%region_20.21.clone | all-reduce | flops 6912 | bytes 55296
  801.1 41.4 %reduce-scatter.29.cloned.1.call-done = f32[24,768]{1,0:T(8,128)} async-done(((f32[768,768]{1,0:T(8,128)}), f32[24,768]{1,0:T(8,128)}) %reduce-scatter.29.cloned.1.call-update) | async-done | bytes 73744
  842.4 104.4 %reduce-scatter.25.cloned.1.call-done = f32[24,768]{1,0:T(8,128)} async-done(((f32[768,768]{1,0:T(8,128)}), f32[24,768]{1,0:T(8,128)}) %reduce-scatter.25.cloned.1.call-update) | async-done | bytes 73744
  946.8 104.3 %reduce-scatter.27.cloned.1.call-done = f32[24,768]{1,0:T(8,128)} async-done(((f32[768,768]{1,0:T(8,128)}), f32[24,768]{1,0:T(8,128)}) %reduce-scatter.27.cloned.1.call-update) | async-done | bytes 73744
  (298 shorter events, 237.6 us)
Async XLA Ops:
  7.2 60.8 %all-gather.11.cloned.1.call-start = ((), (), s32[]{:S(2)}) async-start(), calls=%async_computation.9 | async-start | bytes 1216512 | tf_op jit(solution)/shard_map/all_gather | solution.py:134
  7.9 116.1 %all-gather.13.cloned.1.call-start = ((), (), s32[]{:S(2)}) async-start(), calls=%async_computation.10 | async-start | bytes 1216512 | tf_op jit(solution)/shard_map/all_gather | solution.py:135
  8.7 171.4 %all-gather.9.cloned.1.call-start = ((), (), s32[]{:S(2)}) async-start(), calls=%async_computation.8 | async-start | bytes 1216512 | tf_op jit(solution)/shard_map/all_gather | solution.py:136
  9.4 226.5 %all-gather.15.cloned.1.call-start = ((), (), s32[]{:S(2)}) async-start(), calls=%async_computation.11 | async-start | bytes 1216512 | tf_op jit(solution)/shard_map/all_gather | solution.py:137
  10.0 269.5 %all-gather.19.cloned.1.call-start = ((), (), s32[]{:S(2)}) async-start(), calls=%async_computation.13 | async-start | bytes 2506752 | tf_op jit(solution)/shard_map/all_gather | solution.py:161
  62.5 68.8 %copy-start.26 = (f32[2,256,32]{1,0,2:T(2,128)}, f32[2,256,32]{1,0,2:T(2,128)S(1)}, u32[]{:S(2)}) copy-start(f32[2,256,32]{1,0,2:T(2,128)S(1)} %get-tuple-element.365) | copy-start | bytes 196612
  62.5 68.8 %copy-start.28 = (f32[2,256,32]{1,0,2:T(2,128)}, f32[2,256,32]{1,0,2:T(2,128)S(1)}, u32[]{:S(2)}) copy-start(f32[2,256,32]{1,0,2:T(2,128)S(1)} %get-tuple-element.366) | copy-start | bytes 196612
  71.4 52.7 %copy-start.14 = (bf16[512,768]{1,0:T(8,128)(2,1)S(1)}, bf16[512,768]{1,0:T(8,128)(2,1)}, u32[]{:S(2)}) copy-start(bf16[512,768]{1,0:T(8,128)(2,1)} %param.23) | copy-start | bytes 2359300
  136.3 52.4 %collective-permute-start.1 = (bf16[2,256,12,64]{1,0,3,2:T(2,128)(2,1)}, bf16[2,256,12,64]{1,0,3,2:T(2,128)(2,1)}, u32[]{:S(2)}, u32[]{:S(2)}) collective-permute-start(bf16[2,256,12,64]{1,0,3,2:T(2,128)(2,1)} %pad_maximum_fusion.3), channel_id=1, source_target_pairs={{0,1},{1,0},{2,3},{3,2},{4,5},{5,4},{6,7},{7,6},{8,9},{9,8},{10,11... | collective-permute-start | bytes 2359304 | tf_op jit(solution)/shard_map/ppermute | solution.py:16
  185.5 20.2 %collective-permute-start = (bf16[2,256,12,64]{1,0,3,2:T(2,128)(2,1)}, bf16[2,256,12,64]{1,0,3,2:T(2,128)(2,1)}, u32[]{:S(2)}, u32[]{:S(2)}) collective-permute-start(bf16[2,256,12,64]{1,0,3,2:T(2,128)(2,1)} %convert_element_type.150), channel_id=1, source_target_pairs={{0,1},{1,0},{2,3},{3,2},{4,5},{5,4},{6,7},{7,6},{8,9},{9,8},{10,11... | collective-permute-start | bytes 2359304 | tf_op jit(solution)/shard_map/ppermute | solution.py:16
  187.0 120.4 %all-gather.17.cloned.1.call-start = ((), (), s32[]{:S(2)}) async-start(), calls=%async_computation.12 | async-start | bytes 2359296 | tf_op jit(solution)/shard_map/all_gather | solution.py:205
  240.8 111.3 %all-gather.21.cloned.1.call-start = ((), (), s32[]{:S(2)}) async-start(), calls=%async_computation.14 | async-start | bytes 2506752 | tf_op jit(solution)/shard_map/all_gather | solution.py:162
  241.5 159.8 %reduce-scatter.15.cloned.1.call-start = ((), (), s32[]{:S(2)}) async-start(), calls=%async_computation.15 | async-start | bytes 4718592 | tf_op jit(solution)/shard_map/reduce_scatter | solution.py:213
  359.0 77.2 %all-gather.23.cloned.1.call-start = ((), (), s32[]{:S(2)}) async-start(), calls=%async_computation.16 | async-start | bytes 2359296 | tf_op jit(solution)/shard_map/all_gather | solution.py:226
  408.9 87.2 %reduce-scatter.17.cloned.1.call-start = ((), (), s32[]{:S(2)}) async-start(), calls=%async_computation.17 | async-start | bytes 4718592 | tf_op jit(solution)/shard_map/reduce_scatter | solution.py:233
  452.5 295.9 %reduce-scatter.23.cloned.1.call-start = ((), (), s32[]{:S(2)}) async-start(), calls=%async_computation.20 | async-start | bytes 2506752 | tf_op jit(solution)/shard_map/reduce_scatter | solution.py:240
  459.1 291.0 %reduce-scatter.21.cloned.1.call-start = ((), (), s32[]{:S(2)}) async-start(), calls=%async_computation.19 | async-start | bytes 2506752 | tf_op jit(solution)/shard_map/reduce_scatter | solution.py:237
  465.9 335.2 %reduce-scatter.19.cloned.1.call-start = ((), (), s32[]{:S(2)}) async-start(), calls=%async_computation.18 | async-start | bytes 2433024 | tf_op jit(solution)/shard_map/reduce_scatter | solution.py:280
  511.5 331.0 %reduce-scatter.29.cloned.1.call-start = ((), (), s32[]{:S(2)}) async-start(), calls=%async_computation.23 | async-start | bytes 2433024
  645.8 19.2 %collective-permute-start.3 = (bf16[2,256,12,64]{1,3,2,0:T(8,128)(2,1)S(1)}, bf16[2,256,12,64]{1,3,2,0:T(8,128)(2,1)S(1)}, u32[]{:S(2)}, u32[]{:S(2)}) collective-permute-start(bf16[2,256,12,64]{1,3,2,0:T(8,128)(2,1)S(1)} %slice.78), channel_id=1, source_target_pairs={{0,1},{1,0},{2,3},{3,2},{4,5},{5,4},{6,7},{7,6},{8,9},{9,8},{10,11... | collective-permute-start | bytes 2359304 | tf_op jit(solution)/shard_map/ppermute | solution.py:16
  671.0 275.9 %reduce-scatter.25.cloned.1.call-start = ((), (), s32[]{:S(2)}) async-start(), calls=%async_computation.21 | async-start | bytes 2433024
  673.0 22.5 %collective-permute-start.2 = (bf16[2,256,12,64]{1,0,3,2:T(2,128)(2,1)S(1)}, bf16[2,256,12,64]{1,0,3,2:T(2,128)(2,1)S(1)}, u32[]{:S(2)}, u32[]{:S(2)}) collective-permute-start(bf16[2,256,12,64]{1,0,3,2:T(2,128)(2,1)S(1)} %slice.79), channel_id=1, source_target_pairs={{0,1},{1,0},{2,3},{3,2},{4,5},{5,4},{6,7},{7,6},{8,9},{9,8},{10,11... | collective-permute-start | bytes 2359304 | tf_op jit(solution)/shard_map/ppermute | solution.py:16
  710.0 341.2 %reduce-scatter.27.cloned.1.call-start = ((), (), s32[]{:S(2)}) async-start(), calls=%async_computation.22 | async-start | bytes 2433024
  716.1 78.9 %copy-start.19 = (bf16[96,8,2,256]{3,1,2,0:T(8,128)(2,1)S(1)}, bf16[96,8,2,256]{3,1,2,0:T(8,128)(2,1)}, u32[]{:S(2)}) copy-start(bf16[96,8,2,256]{3,1,2,0:T(8,128)(2,1)} %copy-done.18) | copy-start | bytes 2359300
  (42 other events, 310.4 us)
Sparse Core Ops, SparseCore 0:
  10.9 57.0 all-gather.10
  70.9 53.1 all-gather.12
  127.0 53.0 all-gather.8
  182.9 53.0 all-gather.14
  238.0 41.3 all-gather.18
  281.4 25.9 all-gather.16
  309.7 42.3 all-gather.20
  359.1 42.1 reduce-scatter.14
  409.0 27.1 all-gather.22
  452.7 43.4 reduce-scatter.16
  499.9 63.3 reduce-scatter.22
  566.9 62.3 reduce-scatter.20
  635.2 102.8 reduce-scatter.18
  743.8 98.6 reduce-scatter.28
  848.2 98.6 reduce-scatter.24
  952.5 98.5 reduce-scatter.26
where the time goes:
time: 1070 us; the launch traced here: 1060 us
  waiting for transfers between devices  569 us (53%)
  local copies, waits for them, and re-layouts  157 us (15%)
  blocking collectives  145 us (14%)
  matrix products  117 us (11%)
  other arithmetic  49.2 us (5%)
  between operations  16.2 us (2%)
    unnamed x19, waiting for transfers between devices  254 us
    unnamed x4, blocking collectives  145 us
    dynamic_update_slice x4, local copies, waits for them, and re-layouts, local(): lax.map(attend_back, (query_rot, all_keys, all_values, own_docs, key_docs...  63.5 us
    ppermute x4, waiting for transfers between devices, swapped(): lax.ppermute(shard, axis, [(i, i ^ 1 << bit) for i in range(lax.axis_size...  54.7 us
    all_gather x1, waiting for transfers between devices, local(): lax.all_gather(key_weight, ('wide', 'narrow'), axis=0, tiled=True)  48.6 us
    all_gather x1, waiting for transfers between devices, local(): lax.all_gather(value_weight, ('wide', 'narrow'), axis=0, tiled=True)  42.3 us
    reduce_scatter x1, waiting for transfers between devices, local(): lax.psum_scatter(jnp.dot(block_rows, outer_rows, preferred_element_type=j...  42.2 us
    dynamic_update_slice x4, local copies, waits for them, and re-layouts, local(): lax.map(attend_pack, (query_rot, all_keys, all_values, own_docs, key_docs))  35.1 us
  transfers between devices with their start and end apart: 20, of which 16 were waited for; matrix products, arithmetic and copies ran while one was open for 27% of the time, Pallas kernels for 0%

commit v1 on v0

v1 whole, which is shorter than its diff:
```python
import jax
import jax.numpy as jnp
from jax import lax
from jax.sharding import PartitionSpec as P

D = 768
HEADS = 12
HEAD_DIM = 64

ALL = ("wide", "narrow")
layer_eps = 1e-12
masked_score = -1e30


def swapped(shard, axis, bit):
    return lax.ppermute(shard, axis, [(i, i ^ 1 << bit) for i in range(lax.axis_size(axis))])


def bit_order(total, narrow_n):
    bits = total.bit_length() - 1
    core_bit = narrow_n.bit_length() - 1
    return [b for b in reversed(range(bits)) if b != core_bit] + [core_bit]


def is_pow2(n):
    return n & (n - 1) == 0


def gather_all(shard):
    total = lax.axis_size("wide") * lax.axis_size("narrow")
    narrow_n = lax.axis_size("narrow")
    if not (is_pow2(total) and is_pow2(narrow_n)):
        return lax.all_gather(shard, ALL, axis=0, tiled=False)
    me = lax.axis_index(ALL)
    order = bit_order(total, narrow_n)
    cur = shard
    for b in order:
        other = lax.ppermute(cur, ALL, [(i, i ^ (1 << b)) for i in range(total)])
        bit = (me >> b) & 1
        pick = (jnp.arange(2) == bit).reshape((2,) + (1,) * cur.ndim)
        cur = jnp.where(pick, cur[None], other[None])
    k = len(order)
    perm = [k - 1 - order.index(b) for b in reversed(range(k))]
    cur = cur.transpose(perm + list(range(k, cur.ndim)))
    return cur.reshape((total,) + shard.shape)


def scatter_sum_all(parts):
    total = lax.axis_size("wide") * lax.axis_size("narrow")
    narrow_n = lax.axis_size("narrow")
    if not (is_pow2(total) and is_pow2(narrow_n)):
        return lax.psum_scatter(
            parts.astype(jnp.bfloat16), ALL, scatter_dimension=0, tiled=False
        ).astype(jnp.float32)
    me = lax.axis_index(ALL)
    nbits = total.bit_length() - 1
    cur = parts.reshape((2,) * nbits + parts.shape[1:])
    axes = list(reversed(range(nbits)))
    for b in reversed(bit_order(total, narrow_n)):
        a = axes.index(b)
        bit = (me >> b) & 1
        mine = lax.dynamic_index_in_dim(cur, bit, axis=a, keepdims=False)
        theirs = lax.dynamic_index_in_dim(cur, 1 - bit, axis=a, keepdims=False)
        got = lax.ppermute(
            theirs.astype(jnp.bfloat16), ALL, [(i, i ^ (1 << b)) for i in range(total)]
        )
        cur = mine + got.astype(jnp.float32)
        axes.pop(a)
    return cur


def narrow_gather(rows):
    n = lax.axis_size("narrow")
    if n != 2:
        return lax.all_gather(rows, "narrow", axis=0, tiled=True)
    other = swapped(rows, "narrow", 0)
    first = lax.axis_index("narrow") == 0
    return jnp.where(first, jnp.concatenate([rows, other]), jnp.concatenate([other, rows]))


def narrow_scatter_sum(part):
    n = lax.axis_size("narrow")
    if n != 2:
        return lax.psum_scatter(
            part.astype(jnp.bfloat16), "narrow", scatter_dimension=0, tiled=True
        ).astype(jnp.float32)
    rows = part.shape[0] // 2
    me = lax.axis_index("narrow")
    mine = lax.dynamic_slice_in_dim(part, me * rows, rows, 0)
    theirs = lax.dynamic_slice_in_dim(part, (1 - me) * rows, rows, 0)
    return mine + swapped(theirs.astype(jnp.bfloat16), "narrow", 0).astype(jnp.float32)


def layer_norm(values, gain_vec, shift_vec):
    center = values - jnp.mean(values, axis=-1, keepdims=True)
    spread = jnp.mean(center * center, axis=-1, keepdims=True)
    return center * lax.rsqrt(spread + layer_eps) * gain_vec + shift_vec


def gelu_exact(values):
    return jax.nn.gelu(values, approximate=False)


def rotary_tables(doc_row):
    places = jnp.arange(doc_row.shape[0], dtype=jnp.int32)
    before = jnp.sum((doc_row[None, :] < doc_row[:, None]).astype(jnp.int32), axis=1)
    position = (places - before).astype(jnp.float32)
    frequency = 10000.0 ** (-2.0 * jnp.arange(HEAD_DIM // 2, dtype=jnp.float32) / HEAD_DIM)
    angles = position[:, None] * frequency[None, :]
    return (jnp.cos(angles), jnp.sin(angles))


def rotate(values, cosine, sine_tab):
    half_dim = values.shape[-1] // 2
    first_half = values[..., :half_dim]
    second = values[..., half_dim:]
    return jnp.concatenate(
        [first_half * cosine - second * sine_tab, second * cosine + first_half * sine_tab], axis=-1
    )


def unrotate(values, cosine, sine_tab):
    half_dim = values.shape[-1] // 2
    first_half = values[..., :half_dim]
    second = values[..., half_dim:]
    return jnp.concatenate(
        [first_half * cosine + second * sine_tab, second * cosine - first_half * sine_tab], axis=-1
    )


def contract_rows(left_op, right_op):
    return lax.dot_general(
        left_op, right_op, (((0,), (0,)), ((), ())), preferred_element_type=jnp.float32
    )


def contract_cols(left_op, right_op):
    return lax.dot_general(
        left_op, right_op, (((1,), (1,)), ((), ())), preferred_element_type=jnp.float32
    )


def score_block(query_rot, key_rot, query_docs, key_docs):
    scores = jnp.einsum(
        "pqhd,pkhd->phqk", query_rot, key_rot, preferred_element_type=jnp.float32
    ) * HEAD_DIM ** (-0.5)
    same_doc = query_docs[:, :, None] == key_docs[:, None, :]
    return jnp.where(same_doc[:, None], scores, masked_score)


def attend(query_rot, key_rot, value_low, query_docs, key_docs):
    scores = score_block(query_rot, key_rot, query_docs, key_docs)
    row_peak = jnp.max(scores, axis=-1, keepdims=True)
    exponent = jnp.exp(scores - row_peak)
    totals = jnp.sum(exponent, axis=-1, keepdims=True)
    probability = (exponent / totals).astype(jnp.bfloat16)
    mixed_out = jnp.einsum(
        "phqk,pkhd->pqhd", probability, value_low, preferred_element_type=jnp.float32
    )
    return (mixed_out, row_peak + jnp.log(totals))


def attend_back(query_rot, key_rot, value_low, query_docs, key_docs, logsum, grad_mixed):
    probability = jnp.exp(score_block(query_rot, key_rot, query_docs, key_docs) - logsum)
    grad_values = jnp.einsum(
        "phqk,pqhd->pkhd",
        probability.astype(jnp.bfloat16),
        grad_mixed,
        preferred_element_type=jnp.float32,
    )
    grad_probs = jnp.einsum(
        "pqhd,pkhd->phqk", grad_mixed, value_low, preferred_element_type=jnp.float32
    )
    inner_sum = jnp.sum(probability * grad_probs, axis=-1, keepdims=True)
    grad_scores = (probability * (grad_probs - inner_sum)).astype(jnp.bfloat16)
    grad_query = jnp.einsum(
        "phqk,pkhd->pqhd", grad_scores, key_rot, preferred_element_type=jnp.float32
    ) * HEAD_DIM ** (-0.5)
    grad_keys = jnp.einsum(
        "phqk,pqhd->pkhd", grad_scores, query_rot, preferred_element_type=jnp.float32
    ) * HEAD_DIM ** (-0.5)
    return (grad_query, grad_keys, grad_values)


def local(
    layer_in,
    doc_ids,
    query_weight,
    query_bias,
    key_weight,
    key_bias,
    value_weight,
    value_bias,
    output_weight,
    output_bias,
    attn_gain,
    attn_shift,
    inner_weight,
    inner_bias,
    outer_weight,
    outer_bias,
    ffn_gain,
    ffn_shift,
    cotangent,
):
    wide_n = lax.axis_size("wide")
    total = wide_n * lax.axis_size("narrow")
    share = query_weight.shape[0]
    small_list = (
        query_bias,
        key_bias,
        value_bias,
        output_bias,
        attn_gain,
        attn_shift,
        outer_bias,
        ffn_gain,
        ffn_shift,
    )
    small = jnp.stack(small_list, axis=1)
    small = jnp.pad(small, ((0, 0), (0, 128 - len(small_list))))
    shard = jnp.concatenate([query_weight, key_weight, value_weight, output_weight, small], axis=1)
    full = gather_all(shard).reshape(total * share, shard.shape[1])
    qkv_full = full[:, : 3 * D]
    output_full = full[:, 3 * D : 4 * D]
    vecs = full[:, 4 * D :].astype(jnp.float32)
    (
        query_offset,
        key_offset,
        value_offset,
        output_offset,
        attn_scale,
        attn_offset,
        outer_offset,
        ffn_scale,
        ffn_offset,
    ) = [vecs[:, i] for i in range(len(small_list))]
    qkv_offset = jnp.concatenate([query_offset, key_offset, value_offset])

    ffn_rows, ffn_cols = inner_weight.shape
    bias_n = inner_bias.shape[0]
    bias_k = -(-bias_n // ffn_rows)
    bias_rows = jnp.pad(inner_bias, (0, ffn_rows * bias_k - bias_n)).reshape(ffn_rows, bias_k)
    ffn_shard = jnp.concatenate([inner_weight, outer_weight.T, bias_rows], axis=1)
    ffn_all = lax.all_gather(ffn_shard, "wide", axis=0, tiled=True)
    inner_cols = ffn_all[:, :ffn_cols]
    outer_cols = ffn_all[:, ffn_cols : 2 * ffn_cols]
    inner_offset = ffn_all[:, 2 * ffn_cols :].reshape(wide_n, ffn_rows * bias_k)[:, :bias_n]
    inner_offset = inner_offset.reshape(-1).astype(jnp.float32)

    rows_dev = layer_in.shape[0]
    half_len = doc_ids.shape[1] // 2
    pack_count = rows_dev // half_len
    narrow_place = lax.axis_index("narrow")
    half_bit = narrow_place % 2
    pair_slot = narrow_place // 2
    pack_docs = lax.dynamic_slice_in_dim(doc_ids, pair_slot * pack_count, pack_count, 0)
    cosine, sine_tab = jax.vmap(rotary_tables)(pack_docs)
    cosine = cosine[:, :, None, :]
    sine_tab = sine_tab[:, :, None, :]
    own_start = half_bit * half_len
    far_start = (1 - half_bit) * half_len
    own_cos = lax.dynamic_slice_in_dim(cosine, own_start, half_len, 1)
    own_sin = lax.dynamic_slice_in_dim(sine_tab, own_start, half_len, 1)
    own_docs = lax.dynamic_slice_in_dim(pack_docs, own_start, half_len, 1)
    far_docs = lax.dynamic_slice_in_dim(pack_docs, far_start, half_len, 1)
    key_docs = jnp.concatenate([own_docs, far_docs], axis=1)

    def heads_of(values):
        return values.reshape(pack_count, half_len, HEADS, HEAD_DIM)

    qkv = jnp.dot(layer_in, qkv_full, preferred_element_type=jnp.float32) + qkv_offset
    query_rot = rotate(heads_of(qkv[:, :D]), own_cos, own_sin).astype(jnp.bfloat16)
    key_rot = rotate(heads_of(qkv[:, D : 2 * D]), own_cos, own_sin).astype(jnp.bfloat16)
    value_low = heads_of(qkv[:, 2 * D :]).astype(jnp.bfloat16)
    far_keys, far_values = swapped((key_rot, value_low), "narrow", 0)
    all_keys = jnp.concatenate([key_rot, far_keys], axis=1)
    all_values = jnp.concatenate([value_low, far_values], axis=1)
    mixed_out, logsum = attend(query_rot, all_keys, all_values, own_docs, key_docs)
    mixed_low = mixed_out.reshape(rows_dev, D).astype(jnp.bfloat16)
    attn_out = jnp.dot(mixed_low, output_full, preferred_element_type=jnp.float32) + output_offset
    res_one = layer_in.astype(jnp.float32) + attn_out
    norm_one, norm_pull = jax.vjp(layer_norm, res_one, attn_scale, attn_offset)
    norm_low = norm_one.astype(jnp.bfloat16)
    group_rows = narrow_gather(norm_low)
    inner_pre = jnp.dot(group_rows, inner_cols, preferred_element_type=jnp.float32) + inner_offset
    act_value, gelu_pull = jax.vjp(gelu_exact, inner_pre)
    act_low = act_value.astype(jnp.bfloat16)
    outer_out = narrow_scatter_sum(contract_cols(act_low, outer_cols)) + outer_offset
    res_two = norm_one + outer_out
    layer_out, ffn_pull = jax.vjp(layer_norm, res_two, ffn_scale, ffn_offset)
    grad_two, ffn_gsum, ffn_ssum = ffn_pull(cotangent.astype(jnp.float32))
    grad_outer = grad_two.astype(jnp.bfloat16)
    outer_bsum = jnp.sum(grad_outer.astype(jnp.float32), axis=0)
    group_grads = narrow_gather(grad_outer)
    grad_act = jnp.dot(group_grads, outer_cols, preferred_element_type=jnp.float32)
    grad_inner = gelu_pull(grad_act)[0].astype(jnp.bfloat16)
    outer_wsum_t = contract_rows(group_grads, act_low)
    inner_wsum = contract_rows(group_rows, grad_inner)
    inner_bsum = jnp.sum(grad_inner.astype(jnp.float32), axis=0)
    grad_part = narrow_scatter_sum(contract_cols(grad_inner, inner_cols))
    bsum_rows = jnp.pad(
        inner_bsum.reshape(wide_n, bias_n), ((0, 0), (0, ffn_rows * bias_k - bias_n))
    ).reshape(wide_n * ffn_rows, bias_k)
    ffn_sums = jnp.concatenate([inner_wsum, outer_wsum_t, bsum_rows], axis=1).astype(jnp.bfloat16)
    ffn_mine = lax.psum_scatter(ffn_sums, "wide", scatter_dimension=0, tiled=True)
    ffn_mine = ffn_mine.astype(jnp.float32)
    inner_wgrad = ffn_mine[:, :ffn_cols]
    outer_wgrad = ffn_mine[:, ffn_cols : 2 * ffn_cols].T
    inner_bgrad = ffn_mine[:, 2 * ffn_cols :].reshape(-1)[:bias_n]

    grad_norm = grad_two + grad_part
    grad_one, attn_gsum, attn_ssum = norm_pull(grad_norm)
    grad_attn = grad_one.astype(jnp.bfloat16)
    output_bsum = jnp.sum(grad_attn.astype(jnp.float32), axis=0)
    output_wsum = contract_rows(mixed_low, grad_attn)
    early_small = jnp.stack(
        [output_bsum, attn_gsum, attn_ssum, outer_bsum, ffn_gsum, ffn_ssum], axis=1
    )
    early = jnp.concatenate(
        [output_wsum.reshape(total, share, D), early_small.reshape(total, share, -1)], axis=2
    )
    early_mine = scatter_sum_all(early)

    grad_mixed = heads_of(contract_cols(grad_attn, output_full).astype(jnp.bfloat16))
    grad_qrot, grad_kall, grad_vall = attend_back(
        query_rot, all_keys, all_values, own_docs, key_docs, logsum, grad_mixed
    )
    back_keys, back_values = swapped(
        (
            grad_kall[:, half_len:].astype(jnp.bfloat16),
            grad_vall[:, half_len:].astype(jnp.bfloat16),
        ),
        "narrow",
        0,
    )
    grad_krot = grad_kall[:, :half_len] + back_keys.astype(jnp.float32)
    grad_values = (grad_vall[:, :half_len] + back_values.astype(jnp.float32)).astype(jnp.bfloat16)
    grad_query = unrotate(grad_qrot, own_cos, own_sin).astype(jnp.bfloat16)
    grad_keys = unrotate(grad_krot, own_cos, own_sin).astype(jnp.bfloat16)
    grad_qkv = jnp.concatenate(
        [
            grad_query.reshape(rows_dev, D),
            grad_keys.reshape(rows_dev, D),
            grad_values.reshape(rows_dev, D),
        ],
        axis=1,
    )
    qkv_wsum = contract_rows(layer_in, grad_qkv)
    qkv_bsum = jnp.sum(grad_qkv.astype(jnp.float32), axis=0).reshape(3, D)
    input_grad = grad_one + contract_cols(grad_qkv, qkv_full)
    late = jnp.concatenate(
        [
            qkv_wsum.reshape(total, share, 3 * D),
            qkv_bsum.T.reshape(total, share, 3),
        ],
        axis=2,
    )
    late_mine = scatter_sum_all(late)
    query_wgrad = late_mine[:, :D]
    key_wgrad = late_mine[:, D : 2 * D]
    value_wgrad = late_mine[:, 2 * D : 3 * D]
    query_bgrad = late_mine[:, 3 * D]
    key_bgrad = late_mine[:, 3 * D + 1]
    value_bgrad = late_mine[:, 3 * D + 2]
    output_wgrad = early_mine[:, :D]
    output_bgrad = early_mine[:, D]
    attn_ggrad = early_mine[:, D + 1]
    attn_sgrad = early_mine[:, D + 2]
    outer_bgrad = early_mine[:, D + 3]
    ffn_ggrad = early_mine[:, D + 4]
    ffn_sgrad = early_mine[:, D + 5]
    return (
        layer_out,
        input_grad,
        query_wgrad,
        query_bgrad,
        key_wgrad,
        key_bgrad,
        value_wgrad,
        value_bgrad,
        output_wgrad,
        output_bgrad,
        attn_ggrad,
        attn_sgrad,
        inner_wgrad,
        inner_bgrad,
        outer_wgrad,
        outer_bgrad,
        ffn_ggrad,
        ffn_sgrad,
    )


def solution(mesh):
    return jax.shard_map(
        local,
        mesh=mesh,
        in_specs=(
            P(("wide", "narrow"), None),
            P("wide", None),
            P(("wide", "narrow"), None),
            P(("wide", "narrow")),
            P(("wide", "narrow"), None),
            P(("wide", "narrow")),
            P(("wide", "narrow"), None),
            P(("wide", "narrow")),
            P(("wide", "narrow"), None),
            P(("wide", "narrow")),
            P(("wide", "narrow")),
            P(("wide", "narrow")),
            P("wide", "narrow"),
            P(("narrow", "wide")),
            P("narrow", "wide"),
            P(("wide", "narrow")),
            P(("wide", "narrow")),
            P(("wide", "narrow")),
            P(("wide", "narrow"), None),
        ),
        out_specs=(
            P(("wide", "narrow"), None),
            P(("wide", "narrow"), None),
            P(("wide", "narrow"), None),
            P(("wide", "narrow")),
            P(("wide", "narrow"), None),
            P(("wide", "narrow")),
            P(("wide", "narrow"), None),
            P(("wide", "narrow")),
            P(("wide", "narrow"), None),
            P(("wide", "narrow")),
            P(("wide", "narrow")),
            P(("wide", "narrow")),
            P("wide", "narrow"),
            P(("narrow", "wide")),
            P("narrow", "wide"),
            P(("wide", "narrow")),
            P(("wide", "narrow")),
            P(("wide", "narrow")),
        ),
        check_vma=False,
    )
```

time: 1070 us -> 480 us (0.45)
  waiting for transfers between devices: 569 us -> 201 us
  blocking collectives: 145 us -> 0 us
  local copies, waits for them, and re-layouts: 157 us -> 64.3 us
  starting transfers between devices: 5.22 us -> 36.5 us
  matrix products: 117 us -> 101 us
    unnamed x19 -> x2, waiting for transfers between devices: 254 us -> 0.03 us
    all_gather x8 -> x1, waiting for transfers between devices: 188 us -> 0.01 us  [local(): ffn_all = lax.all_gather(ffn_shard, 'wide', axis=0, tiled=True)]
    unnamed x4 -> x0, blocking collectives: 145 us -> none
    dynamic_update_slice x8 -> x0, local copies, waits for them, and re-layouts: 98.6 us -> none  [the longest x4 63.5 us: local(): lax.map(attend_back, (query_rot, all_keys, all_values, own_docs, key_docs...]
    ppermute x0 -> x15, waiting for transfers between devices: none -> 94.4 us  [the longest x5 52.8 us: gather_all(): other = lax.ppermute(cur, ALL, [(i, i ^ 1 << b) for i in range(total)])]
    reduce_scatter x5 -> x1, waiting for transfers between devices: 72.4 us -> 13.8 us  [local(): lax.psum_scatter(ffn_sums, 'wide', scatter_dimension=0, tiled=True)]
    ppermute x4 -> x8, waiting for transfers between devices: 54.7 us -> 92.6 us  [swapped(): lax.ppermute(shard, axis, [(i, i ^ 1 << bit) for i in range(lax.axis_size...]
    ppermute x0 -> x15, starting transfers between devices: none -> 27.2 us  [the longest x10 19.5 us: scatter_sum_all(): lax.ppermute(theirs.astype(jnp.bfloat16), ALL, [(i, i ^ 1 << b) for i in...]
  transfers between devices with their start and end apart: 20 -> 25, of which waited for: 16 -> 20; matrix products, arithmetic and copies ran while one was open for 27% -> 22% of each run, Pallas kernels for 0% -> 0%
where the time goes in v1:
time: 480 us; the launch traced here: 471 us
  waiting for transfers between devices  201 us (42%)
  matrix products  101 us (21%)
  local copies, waits for them, and re-layouts  64.3 us (13%)
  other arithmetic  52.8 us (11%)
  starting transfers between devices  36.5 us (8%)
  between operations  15.4 us (3%)
    ppermute x8, waiting for transfers between devices, swapped(): lax.ppermute(shard, axis, [(i, i ^ 1 << bit) for i in range(lax.axis_size...  92.6 us
    ppermute x5, waiting for transfers between devices, gather_all(): other = lax.ppermute(cur, ALL, [(i, i ^ 1 << b) for i in range(total)])  52.8 us
    ppermute x10, waiting for transfers between devices, scatter_sum_all(): lax.ppermute(theirs.astype(jnp.bfloat16), ALL, [(i, i ^ 1 << b) for i in...  41.6 us
    dot_general x1, matrix products, local(): jnp.dot(group_rows, inner_cols, preferred_element_type=jnp.float32)  20.6 us
    dot_general x4, matrix products, contract_rows(): lax.dot_general(left_op, right_op, (((0,), (0,)), ((), ())), preferred_el...  19.8 us
    ppermute x10, starting transfers between devices, scatter_sum_all(): lax.ppermute(theirs.astype(jnp.bfloat16), ALL, [(i, i ^ 1 << b) for i in...  19.5 us
    dot_general x4, matrix products, contract_cols(): lax.dot_general(left_op, right_op, (((1,), (1,)), ((), ())), preferred_el...  18.3 us
    unnamed x127, local copies, waits for them, and re-layouts  17.4 us
  transfers between devices with their start and end apart: 25, of which 20 were waited for; matrix products, arithmetic and copies ran while one was open for 22% of the time, Pallas kernels for 0%

profile of v1, /device:TPU:0, one launch (start us, length us, event | category | flops | bytes accessed | tf_op | source)
XLA Modules:
  0.0 471.2 jit_solution(4240909742256947606)
XLA Ops:
  16.1 7.3 %collective-permute-done = bf16[24,3200]{1,0:T(8,128)(2,1)S(1)} collective-permute-done((bf16[24,3200]{1,0:T(8,128)(2,1)S(1)}, bf16[24,3200]{1,0:T(8,128)(2,1)S(1)}, u32[]{:S(2)}, u32[]{:S(2)}) %collective-permute-start) | collective-permute-done | bytes 153632 | tf_op jit(solution)/shard_map/ppermute | solution.py:38
  24.3 7.7 %collective-permute-done.1 = bf16[2,24,3200]{2,1,0:T(8,128)(2,1)S(1)} collective-permute-done((bf16[2,24,3200]{2,1,0:T(8,128)(2,1)S(1)}, bf16[2,24,3200]{2,1,0:T(8,128)(2,1)S(1)}, u32[]{:S(2)}, u32[]{:S(2)}) %collective-permute-start.1) | collective-permute-done | bytes 307232 | tf_op jit(solution)/shard_map/ppermute | solution.py:38
  34.4 12.1 %collective-permute-done.2 = bf16[2,2,24,3200]{3,2,0,1:T(8,128)(2,1)S(1)} collective-permute-done((bf16[2,2,24,3200]{3,2,0,1:T(8,128)(2,1)S(1)}, bf16[2,2,24,3200]{3,2,0,1:T(8,128)(2,1)S(1)}, u32[]{:S(2)}, u32[]{:S(2)}) %collective-permute-start.2) | collective-permute-done | bytes 614432 | tf_op jit(solution)/shard_map/ppermute | solution.py:38
  51.0 22.4 %collective-permute-done.3 = bf16[2,2,2,24,3200]{4,3,0,1,2:T(8,128)(2,1)S(1)} collective-permute-done((bf16[2,2,2,24,3200]{4,3,0,1,2:T(8,128)(2,1)S(1)}, bf16[2,2,2,24,3200]{4,3,0,1,2:T(8,128)(2,1)S(1)}, u32[]{:S(2)}, u32[]{:S(2)}) %collective-permute-start.3) | collective-permute-done | bytes 1228832 | tf_op jit(solution)/shard_map/ppermute | solution.py:38
  100.2 8.8 %collective-permute-done.5 = bf16[2,256,12,64]{1,3,2,0:T(8,128)(2,1)} collective-permute-done((bf16[2,256,12,64]{1,3,2,0:T(8,128)(2,1)}, bf16[2,256,12,64]{1,3,2,0:T(8,128)(2,1)}, u32[]{:S(2)}, u32[]{:S(2)}) %collective-permute-start.5) | collective-permute-done | bytes 786464 | tf_op jit(solution)/shard_map/ppermute | solution.py:16
  110.1 14.8 %collective-permute-done.6 = bf16[2,256,12,64]{1,3,2,0:T(8,128)(2,1)} collective-permute-done((bf16[2,256,12,64]{1,3,2,0:T(8,128)(2,1)}, bf16[2,256,12,64]{1,3,2,0:T(8,128)(2,1)}, u32[]{:S(2)}, u32[]{:S(2)}) %collective-permute-start.6) | collective-permute-done | bytes 786464 | tf_op jit(solution)/shard_map/ppermute | solution.py:16
  144.7 16.4 %collective-permute-done.7 = bf16[512,768]{1,0:T(8,128)(2,1)} collective-permute-done((bf16[512,768]{1,0:T(8,128)(2,1)S(1)}, bf16[512,768]{1,0:T(8,128)(2,1)}, u32[]{:S(2)}, u32[]{:S(2)}) %collective-permute-start.7) | collective-permute-done | bytes 786464 | tf_op jit(solution)/shard_map/ppermute | solution.py:16
  161.1 20.6 %multiply_convert_fusion.1 = (bf16[1024,1536]{1,0:T(8,128)(2,1)S(1)}, f32[1024,1536]{1,0:T(8,128)}, f32[1024,1536]{1,0:T(8,128)}) fusion(f32[1536]{0:T(1024)S(1)} %reshape.279, bf16[768,3074]{1,0:T(8,128)(2,1)} %all-gather.2.cloned.1.call-done, bf16[512,768]{1,0:T(8,128)(2,1)} %collective-permute-done.7, bf16[512,768]{1,0:T(8,128)(2,1)S(1)} %fusion.45, ...), kind=kOutput, calls=%fused_computation.17 | convolution fusion | flops 2526806016 | bytes 19666944 | tf_op jit(solution)/shard_map/dot_general | solution.py:286
  190.3 16.6 %collective-permute-done.8 = bf16[512,768]{1,0:T(8,128)(2,1)S(1)} collective-permute-done((bf16[512,768]{1,0:T(8,128)(2,1)S(1)}, bf16[512,768]{1,0:T(8,128)(2,1)S(1)}, u32[]{:S(2)}, u32[]{:S(2)}) %collective-permute-start.8) | collective-permute-done | bytes 786464 | tf_op jit(solution)/shard_map/ppermute | solution.py:16
  215.4 16.1 %collective-permute-done.9 = bf16[512,768]{1,0:T(8,128)(2,1)} collective-permute-done((bf16[512,768]{1,0:T(8,128)(2,1)}, bf16[512,768]{1,0:T(8,128)(2,1)}, u32[]{:S(2)}, u32[]{:S(2)}) %collective-permute-start.9) | collective-permute-done | bytes 786464 | tf_op jit(solution)/shard_map/ppermute | solution.py:16
  231.5 11.3 %fusion.86 = (bf16[1536]{0:T(1024)(128)(2,1)}, bf16[1024,1536]{1,0:T(8,128)(2,1)S(1)}) fusion(f32[1024,1536]{1,0:T(8,128)} %get-tuple-element.54, bf16[768,3074]{1,0:T(8,128)(2,1)} %all-gather.2.cloned.1.call-done, bf16[512,768]{1,0:T(8,128)(2,1)} %collective-permute-done.9, bf16[512,768]{1,0:T(8,128)(2,1)} %get-tuple-element.43, pred[]{:T(512)S(6)} %eq.93, ...), kind=kOutput, calls=%fused_computation.230 | convolution fusion | flops 2448161280 | bytes 19672064 | tf_op jit(solution)/shard_map/dot_general | solution.py:296
  242.8 5.4 %fusion.28 = f32[1024,768]{1,0:T(8,128)S(1)} fusion(bf16[1024,1536]{1,0:T(8,128)(2,1)S(1)} %get-tuple-element.91, bf16[768,3074]{1,0:T(8,128)(2,1)} %all-gather.2.cloned.1.call-done), kind=kOutput, calls=%fused_computation.61 | convolution fusion | flops 2415919104 | bytes 8650752 | tf_op jit(solution)/shard_map/dot_general | solution.py:138
  259.7 7.3 %convolution_convert_fusion = bf16[768,1536]{1,0:T(8,128)(2,1)} fusion(bf16[1024,1536]{1,0:T(8,128)(2,1)} %copy-done.54, bf16[512,768]{1,0:T(8,128)(2,1)} %collective-permute-done.9, bf16[512,768]{1,0:T(8,128)(2,1)} %get-tuple-element.43, pred[]{:T(512)S(6)} %eq.93), kind=kOutput, calls=%fused_computation.43 | convolution fusion | flops 2424176640 | bytes 7077889 | tf_op jit(solution)/shard_map/dot_general | solution.py:132
  275.6 10.2 %multiply_reduce_fusion = (f32[2,12,256]{2,1,0:T(8,128)S(1)}, f32[2,12,256,512]{3,2,1,0:T(8,128)}) fusion(f32[2,12,256]{2,1,0:T(8,128)} %log_add_fusion, f32[2,12,256,512]{3,2,1,0:T(8,128)} %copy-done, pred[2,256,512]{2,1,0:T(8,128)(4,1)S(1)} %broadcast_compare_fusion, bf16[2,512,12,64]{1,3,2,0:T(8,128)(2,1)S(1)} %copy-done.16, ...), kind=kOutput, calls=%fused_computation.1 | convolution fusion | flops 418375680 | bytes 27836416 | tf_op jit(solution)/shard_map/pqhd,pkhd->phqk/dot_general | solution.py:171
  285.8 9.9 %multiply_convert_fusion = bf16[2,12,256,512]{3,2,1,0:T(8,128)(2,1)S(1)} fusion(f32[2,12,256,512]{3,2,1,0:T(8,128)} %get-tuple-element.89, f32[2,12,256]{2,1,0:T(8,128)S(1)} %get-tuple-element.88, f32[2,12,256]{2,1,0:T(8,128)S(1)} %copy-done.34, f32[2,12,256,512]{3,2,1,0:T(8,128)} %copy-done, pred[2,256,512]{2,1,0:T(8,128)(4,1)S(1)} %broadcast_compare_fusion), kind=kLoop, calls=%fused_computation | loop fusion | flops 18874368 | bytes 31768576 | tf_op jit(solution)/shard_map/convert_element_type | solution.py:175
  306.9 11.8 %collective-permute-done.11 = bf16[2,256,12,64]{1,3,2,0:T(8,128)(2,1)} collective-permute-done((bf16[2,256,12,64]{1,3,2,0:T(8,128)(2,1)}, bf16[2,256,12,64]{1,3,2,0:T(8,128)(2,1)}, u32[]{:S(2)}, u32[]{:S(2)}) %collective-permute-start.11) | collective-permute-done | bytes 786464 | tf_op jit(solution)/shard_map/ppermute | solution.py:16
  322.8 7.8 %collective-permute-done.12 = bf16[2,256,12,64]{1,3,2,0:T(8,128)(2,1)S(1)} collective-permute-done((bf16[2,256,12,64]{1,3,2,0:T(8,128)(2,1)S(1)}, bf16[2,256,12,64]{1,3,2,0:T(8,128)(2,1)S(1)}, u32[]{:S(2)}, u32[]{:S(2)}) %collective-permute-start.12) | collective-permute-done | bytes 786464 | tf_op jit(solution)/shard_map/ppermute | solution.py:16
  360.2 5.6 %pad_maximum_fusion = bf16[768,3074]{1,0:T(8,128)(2,1)} fusion(bf16[768,2]{1,0:T(8,128)(2,1)} %reshape.277, bf16[768,1536]{1,0:T(8,128)(2,1)} %convolution_convert_fusion, bf16[768,1536]{1,0:T(8,128)(2,1)} %convolution_convert_fusion.1), kind=kLoop, calls=%fused_computation.32 | loop fusion | flops 14164992 | bytes 9443328 | tf_op jit(solution)/shard_map/concatenate | solution.py:305
  388.7 10.3 %collective-permute-done.14 = bf16[2,2,2,24,2307]{4,3,0,1,2:T(8,128)(2,1)S(1)} collective-permute-done((bf16[2,2,2,24,2307]{4,3,0,1,2:T(8,128)(2,1)}, bf16[2,2,2,24,2307]{4,3,0,1,2:T(8,128)(2,1)S(1)}, u32[]{:S(2)}, u32[]{:S(2)}) %collective-permute-start.14) | collective-permute-done | bytes 885920 | tf_op jit(solution)/shard_map/ppermute | solution.py:64
  407.5 6.9 %collective-permute-start.22 = (bf16[24,774]{1,0:T(8,128)(2,1)S(1)}, bf16[24,774]{1,0:T(8,128)(2,1)S(1)}, u32[]{:S(2)}, u32[]{:S(2)}) collective-permute-start(bf16[24,774]{1,0:T(8,128)(2,1)S(1)} %fusion.62), channel_id=1, source_target_pairs={{0,16},{1,17},{2,18},{3,19},{4,20},{5,21},{6,22},{7,23},{8,24},{9,... | collective-permute-start | bytes 111464 | tf_op jit(solution)/shard_map/ppermute | solution.py:64
  414.4 8.8 %collective-permute-done.15 = bf16[2,2,24,2307]{3,2,0,1:T(8,128)(2,1)S(1)} collective-permute-done((bf16[2,2,24,2307]{3,2,0,1:T(8,128)(2,1)S(1)}, bf16[2,2,24,2307]{3,2,0,1:T(8,128)(2,1)S(1)}, u32[]{:S(2)}, u32[]{:S(2)}) %collective-permute-start.15) | collective-permute-done | bytes 442976 | tf_op jit(solution)/shard_map/ppermute | solution.py:64
  425.5 10.2 %collective-permute-done.16 = bf16[2,24,2307]{2,1,0:T(8,128)(2,1)S(1)} collective-permute-done((bf16[2,24,2307]{2,1,0:T(8,128)(2,1)S(1)}, bf16[2,24,2307]{2,1,0:T(8,128)(2,1)S(1)}, u32[]{:S(2)}, u32[]{:S(2)}) %collective-permute-start.16) | collective-permute-done | bytes 221504 | tf_op jit(solution)/shard_map/ppermute | solution.py:64
  438.3 5.9 %collective-permute-done.17 = bf16[24,2307]{1,0:T(8,128)(2,1)S(1)} collective-permute-done((bf16[24,2307]{1,0:T(8,128)(2,1)S(1)}, bf16[24,2307]{1,0:T(8,128)(2,1)S(1)}, u32[]{:S(2)}, u32[]{:S(2)}) %collective-permute-start.17) | collective-permute-done | bytes 110768 | tf_op jit(solution)/shard_map/ppermute | solution.py:64
  445.6 13.8 %reduce-scatter.2.cloned.1.call-done = bf16[48,3074]{1,0:T(8,128)(2,1)} async-done(((bf16[768,3074]{1,0:T(8,128)(2,1)}), bf16[48,3074]{1,0:T(8,128)(2,1)}) %reduce-scatter.2.cloned.1.call-update) | async-done | bytes 295120 | tf_op jit(solution)/shard_map/reduce_scatter | solution.py:306
  (295 shorter events, 187.8 us)
Async XLA Ops:
  7.2 136.3 %all-gather.2.cloned.1.call-start = ((), (), s32[]{:S(2)}) async-start(), calls=%async_computation.1 | async-start | bytes 5222400 | tf_op jit(solution)/shard_map/all_gather | solution.py:245
  11.9 11.4 %collective-permute-start = (bf16[24,3200]{1,0:T(8,128)(2,1)S(1)}, bf16[24,3200]{1,0:T(8,128)(2,1)S(1)}, u32[]{:S(2)}, u32[]{:S(2)}) collective-permute-start(bf16[24,3200]{1,0:T(8,128)(2,1)S(1)} %constant_dynamic-update-slice_fusion), channel_id=1, source_target_pairs={{0,16},{1,17},{2,18},{3,19},{4,20},{5,21},{6,22},{7,23},{8,24},{9,... | collective-permute-start | bytes 460808 | tf_op jit(solution)/shard_map/ppermute | solution.py:38
  23.5 8.5 %collective-permute-start.1 = (bf16[2,24,3200]{2,1,0:T(8,128)(2,1)S(1)}, bf16[2,24,3200]{2,1,0:T(8,128)(2,1)S(1)}, u32[]{:S(2)}, u32[]{:S(2)}) collective-permute-start(bf16[2,24,3200]{2,1,0:T(8,128)(2,1)S(1)} %broadcast_select_fusion.5), channel_id=1, source_target_pairs={{0,8},{1,9},{2,10},{3,11},{4,12},{5,13},{6,14},{7,15},{8,0},{9,1},... | collective-permute-start | bytes 921608 | tf_op jit(solution)/shard_map/ppermute | solution.py:38
  32.3 14.2 %collective-permute-start.2 = (bf16[2,2,24,3200]{3,2,0,1:T(8,128)(2,1)S(1)}, bf16[2,2,24,3200]{3,2,0,1:T(8,128)(2,1)S(1)}, u32[]{:S(2)}, u32[]{:S(2)}) collective-permute-start(bf16[2,2,24,3200]{3,2,0,1:T(8,128)(2,1)S(1)} %broadcast_select_fusion.4), channel_id=1, source_target_pairs={{0,4},{1,5},{2,6},{3,7},{4,0},{5,1},{6,2},{7,3},{8,12},{9,13},{10,... | collective-permute-start | bytes 1843208 | tf_op jit(solution)/shard_map/ppermute | solution.py:38
  46.9 26.5 %collective-permute-start.3 = (bf16[2,2,2,24,3200]{4,3,0,1,2:T(8,128)(2,1)S(1)}, bf16[2,2,2,24,3200]{4,3,0,1,2:T(8,128)(2,1)S(1)}, u32[]{:S(2)}, u32[]{:S(2)}) collective-permute-start(bf16[2,2,2,24,3200]{4,3,0,1,2:T(8,128)(2,1)S(1)} %broadcast_select_fusion.2), channel_id=1, source_target_pairs={{0,1},{1,0},{2,3},{3,2},{4,5},{5,4},{6,7},{7,6},{8,9},{9,8},{10,11... | collective-permute-start | bytes 3686408 | tf_op jit(solution)/shard_map/ppermute | solution.py:38
  50.0 409.5 %reduce-scatter.2.cloned.1.call-start = ((), (), s32[]{:S(2)}) async-start(), calls=%async_computation.2 | async-start | bytes 5222400 | tf_op jit(solution)/shard_map/reduce_scatter | solution.py:306
  88.2 20.7 %collective-permute-start.5 = (bf16[2,256,12,64]{1,3,2,0:T(8,128)(2,1)}, bf16[2,256,12,64]{1,3,2,0:T(8,128)(2,1)}, u32[]{:S(2)}, u32[]{:S(2)}) collective-permute-start(bf16[2,256,12,64]{1,3,2,0:T(8,128)(2,1)} %get-tuple-element.70), channel_id=1, source_target_pairs={{0,1},{1,0},{2,3},{3,2},{4,5},{5,4},{6,7},{7,6},{8,9},{9,8},{10,11... | collective-permute-start | bytes 2359304 | tf_op jit(solution)/shard_map/ppermute | solution.py:16
  99.2 25.8 %collective-permute-start.6 = (bf16[2,256,12,64]{1,3,2,0:T(8,128)(2,1)}, bf16[2,256,12,64]{1,3,2,0:T(8,128)(2,1)}, u32[]{:S(2)}, u32[]{:S(2)}) collective-permute-start(bf16[2,256,12,64]{1,3,2,0:T(8,128)(2,1)} %pad_maximum_fusion.3), channel_id=1, source_target_pairs={{0,1},{1,0},{2,3},{3,2},{4,5},{5,4},{6,7},{7,6},{8,9},{9,8},{10,11... | collective-permute-start | bytes 2359304 | tf_op jit(solution)/shard_map/ppermute | solution.py:16
  142.2 18.9 %collective-permute-start.7 = (bf16[512,768]{1,0:T(8,128)(2,1)S(1)}, bf16[512,768]{1,0:T(8,128)(2,1)}, u32[]{:S(2)}, u32[]{:S(2)}) collective-permute-start(bf16[512,768]{1,0:T(8,128)(2,1)S(1)} %fusion.45), channel_id=1, source_target_pairs={{0,1},{1,0},{2,3},{3,2},{4,5},{5,4},{6,7},{7,6},{8,9},{9,8},{10,11... | collective-permute-start | bytes 2359304 | tf_op jit(solution)/shard_map/ppermute | solution.py:16
  189.0 17.9 %collective-permute-start.8 = (bf16[512,768]{1,0:T(8,128)(2,1)S(1)}, bf16[512,768]{1,0:T(8,128)(2,1)S(1)}, u32[]{:S(2)}, u32[]{:S(2)}) collective-permute-start(bf16[512,768]{1,0:T(8,128)(2,1)S(1)} %dynamic-slice_convert_fusion.2), channel_id=1, source_target_pairs={{0,1},{1,0},{2,3},{3,2},{4,5},{5,4},{6,7},{7,6},{8,9},{9,8},{10,11... | collective-permute-start | bytes 2359304 | tf_op jit(solution)/shard_map/ppermute | solution.py:16
  214.1 17.3 %collective-permute-start.9 = (bf16[512,768]{1,0:T(8,128)(2,1)}, bf16[512,768]{1,0:T(8,128)(2,1)}, u32[]{:S(2)}, u32[]{:S(2)}) collective-permute-start(bf16[512,768]{1,0:T(8,128)(2,1)} %get-tuple-element.43), channel_id=1, source_target_pairs={{0,1},{1,0},{2,3},{3,2},{4,5},{5,4},{6,7},{7,6},{8,9},{9,8},{10,11... | collective-permute-start | bytes 2359304 | tf_op jit(solution)/shard_map/ppermute | solution.py:16
  250.9 16.5 %collective-permute-start.10 = (bf16[512,768]{1,0:T(8,128)(2,1)}, bf16[512,768]{1,0:T(8,128)(2,1)}, u32[]{:S(2)}, u32[]{:S(2)}) collective-permute-start(bf16[512,768]{1,0:T(8,128)(2,1)} %dynamic-slice_convert_fusion.1), channel_id=1, source_target_pairs={{0,1},{1,0},{2,3},{3,2},{4,5},{5,4},{6,7},{7,6},{8,9},{9,8},{10,11... | collective-permute-start | bytes 2359304 | tf_op jit(solution)/shard_map/ppermute | solution.py:16
  298.0 20.7 %collective-permute-start.11 = (bf16[2,256,12,64]{1,3,2,0:T(8,128)(2,1)}, bf16[2,256,12,64]{1,3,2,0:T(8,128)(2,1)}, u32[]{:S(2)}, u32[]{:S(2)}) collective-permute-start(bf16[2,256,12,64]{1,3,2,0:T(8,128)(2,1)} %slice.290), channel_id=1, source_target_pairs={{0,1},{1,0},{2,3},{3,2},{4,5},{5,4},{6,7},{7,6},{8,9},{9,8},{10,11... | collective-permute-start | bytes 2359304 | tf_op jit(solution)/shard_map/ppermute | solution.py:16
  303.0 27.6 %collective-permute-start.12 = (bf16[2,256,12,64]{1,3,2,0:T(8,128)(2,1)S(1)}, bf16[2,256,12,64]{1,3,2,0:T(8,128)(2,1)S(1)}, u32[]{:S(2)}, u32[]{:S(2)}) collective-permute-start(bf16[2,256,12,64]{1,3,2,0:T(8,128)(2,1)S(1)} %slice.289), channel_id=1, source_target_pairs={{0,1},{1,0},{2,3},{3,2},{4,5},{5,4},{6,7},{7,6},{8,9},{9,8},{10,11... | collective-permute-start | bytes 2359304 | tf_op jit(solution)/shard_map/ppermute | solution.py:16
  342.4 27.6 %collective-permute-start.13 = (bf16[2,2,2,2,24,2307]{5,4,0,1,2,3:T(8,128)(2,1)}, bf16[2,2,2,2,24,2307]{5,4,0,1,2,3:T(8,128)(2,1)}, u32[]{:S(2)}, u32[]{:S(2)}) collective-permute-start(bf16[2,2,2,2,24,2307]{5,4,0,1,2,3:T(8,128)(2,1)} %fusion.37), channel_id=1, source_target_pairs={{0,2},{1,3},{2,0},{3,1},{4,6},{5,7},{6,4},{7,5},{8,10},{9,11},{10,... | collective-permute-start | bytes 5315336 | tf_op jit(solution)/shard_map/ppermute | solution.py:64
  359.7 6.2 %collective-permute-start.18 = (bf16[2,2,2,2,24,774]{5,4,3,2,1,0:T(8,128)(2,1)}, bf16[2,2,2,2,24,774]{5,4,3,2,1,0:T(8,128)(2,1)}, u32[]{:S(2)}, u32[]{:S(2)}) collective-permute-start(bf16[2,2,2,2,24,774]{5,4,3,2,1,0:T(8,128)(2,1)} %fusion.54), channel_id=1, source_target_pairs={{0,2},{1,3},{2,0},{3,1},{4,6},{5,7},{6,4},{7,5},{8,10},{9,11},{10,... | collective-permute-start | bytes 1783304 | tf_op jit(solution)/shard_map/ppermute | solution.py:64
  368.9 10.4 %collective-permute-start.19 = (bf16[2,2,2,24,774]{4,3,2,1,0:T(8,128)(2,1)S(1)}, bf16[2,2,2,24,774]{4,3,2,1,0:T(8,128)(2,1)S(1)}, u32[]{:S(2)}, u32[]{:S(2)}) collective-permute-start(bf16[2,2,2,24,774]{4,3,2,1,0:T(8,128)(2,1)S(1)} %fusion.57), channel_id=1, source_target_pairs={{0,1},{1,0},{2,3},{3,2},{4,5},{5,4},{6,7},{7,6},{8,9},{9,8},{10,11... | collective-permute-start | bytes 891656 | tf_op jit(solution)/shard_map/ppermute | solution.py:64
  375.9 23.1 %collective-permute-start.14 = (bf16[2,2,2,24,2307]{4,3,0,1,2:T(8,128)(2,1)}, bf16[2,2,2,24,2307]{4,3,0,1,2:T(8,128)(2,1)S(1)}, u32[]{:S(2)}, u32[]{:S(2)}) collective-permute-start(bf16[2,2,2,24,2307]{4,3,0,1,2:T(8,128)(2,1)} %fusion.48), channel_id=1, source_target_pairs={{0,1},{1,0},{2,3},{3,2},{4,5},{5,4},{6,7},{7,6},{8,9},{9,8},{10,11... | collective-permute-start | bytes 2657672 | tf_op jit(solution)/shard_map/ppermute | solution.py:64
  379.4 5.5 %collective-permute-start.20 = (bf16[2,2,24,774]{3,2,1,0:T(8,128)(2,1)S(1)}, bf16[2,2,24,774]{3,2,1,0:T(8,128)(2,1)S(1)}, u32[]{:S(2)}, u32[]{:S(2)}) collective-permute-start(bf16[2,2,24,774]{3,2,1,0:T(8,128)(2,1)S(1)} %fusion.59), channel_id=1, source_target_pairs={{0,4},{1,5},{2,6},{3,7},{4,0},{5,1},{6,2},{7,3},{8,12},{9,13},{10,... | collective-permute-start | bytes 445832 | tf_op jit(solution)/shard_map/ppermute | solution.py:64
  385.0 22.5 %collective-permute-start.21 = (bf16[2,24,774]{2,1,0:T(8,128)(2,1)S(1)}, bf16[2,24,774]{2,1,0:T(8,128)(2,1)S(1)}, u32[]{:S(2)}, u32[]{:S(2)}) collective-permute-start(bf16[2,24,774]{2,1,0:T(8,128)(2,1)S(1)} %fusion.61), channel_id=1, source_target_pairs={{0,8},{1,9},{2,10},{3,11},{4,12},{5,13},{6,14},{7,15},{8,0},{9,1},... | collective-permute-start | bytes 222920 | tf_op jit(solution)/shard_map/ppermute | solution.py:64
  400.7 22.5 %collective-permute-start.15 = (bf16[2,2,24,2307]{3,2,0,1:T(8,128)(2,1)S(1)}, bf16[2,2,24,2307]{3,2,0,1:T(8,128)(2,1)S(1)}, u32[]{:S(2)}, u32[]{:S(2)}) collective-permute-start(bf16[2,2,24,2307]{3,2,0,1:T(8,128)(2,1)S(1)} %fusion.56), channel_id=1, source_target_pairs={{0,4},{1,5},{2,6},{3,7},{4,0},{5,1},{6,2},{7,3},{8,12},{9,13},{10,... | collective-permute-start | bytes 1328840 | tf_op jit(solution)/shard_map/ppermute | solution.py:64
  407.5 17.4 %collective-permute-start.22 = (bf16[24,774]{1,0:T(8,128)(2,1)S(1)}, bf16[24,774]{1,0:T(8,128)(2,1)S(1)}, u32[]{:S(2)}, u32[]{:S(2)}) collective-permute-start(bf16[24,774]{1,0:T(8,128)(2,1)S(1)} %fusion.62), channel_id=1, source_target_pairs={{0,16},{1,17},{2,18},{3,19},{4,20},{5,21},{6,22},{7,23},{8,24},{9,... | collective-permute-start | bytes 111464 | tf_op jit(solution)/shard_map/ppermute | solution.py:64
  423.3 12.4 %collective-permute-start.16 = (bf16[2,24,2307]{2,1,0:T(8,128)(2,1)S(1)}, bf16[2,24,2307]{2,1,0:T(8,128)(2,1)S(1)}, u32[]{:S(2)}, u32[]{:S(2)}) collective-permute-start(bf16[2,24,2307]{2,1,0:T(8,128)(2,1)S(1)} %fusion.58), channel_id=1, source_target_pairs={{0,8},{1,9},{2,10},{3,11},{4,12},{5,13},{6,14},{7,15},{8,0},{9,1},... | collective-permute-start | bytes 664424 | tf_op jit(solution)/shard_map/ppermute | solution.py:64
  435.8 8.4 %collective-permute-start.17 = (bf16[24,2307]{1,0:T(8,128)(2,1)S(1)}, bf16[24,2307]{1,0:T(8,128)(2,1)S(1)}, u32[]{:S(2)}, u32[]{:S(2)}) collective-permute-start(bf16[24,2307]{1,0:T(8,128)(2,1)S(1)} %fusion.60), channel_id=1, source_target_pairs={{0,16},{1,17},{2,18},{3,19},{4,20},{5,21},{6,22},{7,23},{8,24},{9,... | collective-permute-start | bytes 332216 | tf_op jit(solution)/shard_map/ppermute | solution.py:64
  (59 other events, 676.5 us)
Sparse Core Ops, SparseCore 0:
  50.1 56.0 all-gather.1
  366.0 93.4 reduce-scatter.1
